TPU v7x, 32 devices: a whole 2x2x4 slice. The times are simulated.
32 devices in a mesh: dp: 8 (over z, y), query: 4 (over x, core).
Axes of the slice: x: 2, y: 2, z: 4, core: 2. Of those that a mesh axis runs over, the one named last changes fastest.
Arguments:
- sensors: bfloat16 [3072, 4096], P('dp'), may hold values from -8 to 8
- query_index: int32 [2, 8192], P(None, 'query'), may hold values from 0 to 127
- targets: bfloat16 [3072, 8192], P('dp', 'query'), may hold values from -6 to 6
- w_one: bfloat16 [4096, 1024], P(None, 'query'), may hold values from -0.09375 to 0.09375
- b_one: float32 [1024], P('query'), may hold values from -3 to 3
- w_two: bfloat16 [1024, 512], P('query'), may hold values from -0.1875 to 0.1875
- b_two: float32 [512], replicated, may hold values from -3 to 3
- v_one: float32 [2, 512], replicated, may hold values from -4 to 4
- c_one: float32 [512], replicated, may hold values from -3 to 3
- v_two: bfloat16 [512, 512], replicated, may hold values from -0.25 to 0.25
- c_two: float32 [512], replicated, may hold values from -3 to 3
- v_three: bfloat16 [512, 512], replicated, may hold values from -0.25 to 0.25
- c_three: float32 [512], replicated, may hold values from -3 to 3
Outputs:
- loss: float32 [], replicated
- grad_w_one: float32 [4096, 1024], P('dp', 'query')
- grad_b_one: float32 [1024], P('query')
- grad_w_two: float32 [1024, 512], P('query', 'dp')
- grad_b_two: float32 [512], replicated
- grad_v_one: float32 [2, 512], replicated
- grad_c_one: float32 [512], replicated
- grad_v_two: float32 [512, 512], replicated
- grad_c_two: float32 [512], replicated
- grad_v_three: float32 [512, 512], replicated
- grad_c_three: float32 [512], replicated
All inputs are finite; a program needn't handle non-finite values.
Results may differ from a plain program's by a relative error of at most 0.00075.
Values may be sent and summed in bfloat16 or wider, within the bound.
A program may use at most 128 MiB of HBM per device.

v0:
```python
import math
import jax
import jax.numpy as jnp
from jax import lax
from jax.sharding import PartitionSpec as P

GRID = 128


def contract_rows(left, right, precision=None):
    return lax.dot_general(
        left,
        right,
        (((0,), (0,)), ((), ())),
        precision=precision,
        preferred_element_type=jnp.float32,
    )


def contract_cols(left, right, precision=None):
    return lax.dot_general(
        left,
        right,
        (((1,), (1,)), ((), ())),
        precision=precision,
        preferred_element_type=jnp.float32,
    )


def trunk_forward(coords, v_one, c_one, v_two, c_two, v_three, c_three):
    first_act = jnp.tanh(
        coords[0][:, None] * v_one[0][None, :] + coords[1][:, None] * v_one[1][None, :] + c_one
    )
    first_b = first_act.astype(jnp.bfloat16)
    second_act = jnp.tanh(jnp.dot(first_b, v_two, preferred_element_type=jnp.float32) + c_two)
    second_b = second_act.astype(jnp.bfloat16)
    basis_full = jnp.dot(second_b, v_three, preferred_element_type=jnp.float32) + c_three
    return (first_act, first_b, second_act, second_b, basis_full.astype(jnp.bfloat16))


def trunk_backward(coords, first_act, first_b, second_act, second_b, grad_basis, v_two, v_three):
    grad_basis_b = grad_basis.astype(jnp.bfloat16)
    grad_v_three = contract_rows(second_b, grad_basis_b)
    grad_c_three = jnp.sum(grad_basis, axis=0)
    grad_second = contract_cols(grad_basis_b, v_three) * (1.0 - second_act * second_act)
    grad_second_b = grad_second.astype(jnp.bfloat16)
    grad_v_two = contract_rows(first_b, grad_second_b)
    grad_c_two = jnp.sum(grad_second, axis=0)
    grad_first = contract_cols(grad_second_b, v_two) * (1.0 - first_act * first_act)
    grad_v_one = jnp.dot(
        coords, grad_first, precision=lax.Precision.HIGHEST, preferred_element_type=jnp.float32
    )
    grad_c_one = jnp.sum(grad_first, axis=0)
    return (grad_v_one, grad_c_one, grad_v_two, grad_c_two, grad_v_three, grad_c_three)


def local(
    sensors,
    query_index,
    targets,
    w_one,
    b_one,
    w_two,
    b_two,
    v_one,
    c_one,
    v_two,
    c_two,
    v_three,
    c_three,
):
    dp_count = lax.axis_size("dp")
    func_rows = sensors.shape[0]
    query_rows = query_index.shape[1]
    count_all = func_rows * dp_count * query_rows * lax.axis_size("query")
    grad_scale = 64.0 / math.sqrt(count_all)
    inv_scale = 1.0 / math.sqrt(w_two.shape[1])
    coords_all = query_index.astype(jnp.float32) / (GRID - 1)
    hidden = jnp.tanh(jnp.dot(sensors, w_one, preferred_element_type=jnp.float32) + b_one)
    hidden_b = hidden.astype(jnp.bfloat16)
    partial_value = jnp.dot(hidden_b, w_two, preferred_element_type=jnp.float32)
    coeffs = lax.psum(partial_value, "query") + b_two
    coeffs_b = coeffs.astype(jnp.bfloat16)
    row_share = query_rows // dp_count
    coords_mine = lax.dynamic_slice_in_dim(
        coords_all, lax.axis_index("dp") * row_share, row_share, 1
    )
    first_act, first_b, second_act, second_b, basis_b = trunk_forward(
        coords_mine, v_one, c_one, v_two, c_two, v_three, c_three
    )
    basis_all = lax.all_gather(basis_b, "dp", axis=0, tiled=True)
    prediction = contract_cols(coeffs_b, basis_all) * inv_scale
    misfit = prediction - targets.astype(jnp.float32)
    loss_part = jnp.sum(misfit * misfit)
    misfit_b = (misfit * grad_scale).astype(jnp.bfloat16)
    grad_coeffs = lax.psum(
        jnp.dot(misfit_b, basis_all, preferred_element_type=jnp.float32) * inv_scale, "query"
    )
    grad_coeffs_b = grad_coeffs.astype(jnp.bfloat16)
    loss_value = lax.psum(loss_part, ("dp", "query")) / count_all
    columns = misfit_b
    grad_basis = lax.psum_scatter(
        contract_rows(columns, coeffs_b) * inv_scale, "dp", scatter_dimension=0, tiled=True
    )
    trunk_parts = trunk_backward(
        coords_mine, first_act, first_b, second_act, second_b, grad_basis, v_two, v_three
    )
    grad_w_two_part = contract_rows(hidden_b, grad_coeffs_b)
    grad_pre = contract_cols(grad_coeffs_b, w_two) * (1.0 - hidden * hidden)
    grad_pre_b = grad_pre.astype(jnp.bfloat16)
    grad_b_one, grad_b_two = lax.psum(
        (jnp.sum(grad_pre, axis=0), jnp.sum(grad_coeffs, axis=0)), "dp"
    )
    columns = sensors
    grad_w_one = lax.psum_scatter(
        contract_rows(columns, grad_pre_b), "dp", scatter_dimension=0, tiled=True
    )
    grad_w_two = lax.psum_scatter(grad_w_two_part, "dp", scatter_dimension=1, tiled=True)
    trunk_sums = lax.psum(
        (
            trunk_parts[0],
            trunk_parts[1],
            trunk_parts[2],
            trunk_parts[3],
            trunk_parts[4],
            trunk_parts[5],
        ),
        ("dp", "query"),
    )
    return (
        loss_value,
        grad_w_one,
        grad_b_one,
        grad_w_two,
        grad_b_two,
        trunk_sums[0],
        trunk_sums[1],
        trunk_sums[2],
        trunk_sums[3],
        trunk_sums[4],
        trunk_sums[5],
    )


def solution(mesh):
    placed = (
        P("dp", None),
        P(None, "query"),
        P("dp", "query"),
        P(None, "query"),
        P("query"),
        P("query", None),
        P(),
        P(),
        P(),
        P(),
        P(),
        P(),
        P(),
    )
    return jax.shard_map(
        local,
        mesh=mesh,
        in_specs=placed,
        out_specs=(
            P(),
            P("dp", "query"),
            P("query"),
            P("query", "dp"),
            P(),
            P(),
            P(),
            P(),
            P(),
            P(),
            P(),
        ),
        check_vma=False,
    )
```

profile of v0, /device:TPU:0, one launch (start us, length us, event | category | flops | bytes accessed | tf_op | source)
XLA Modules:
  0.0 356.2 jit_solution(2929589968027508688)
XLA Ops:
  8.1 1.8 copy-done
  9.9 2.6 fusion.2
  12.6 1.1 fusion.19
  14.5 0.8 fusion.24
  15.3 1.4 fusion
  16.7 0.8 copy-done.2
  17.5 2.1 fusion.1
  19.6 32.0 %all-reduce.7.cloned.1.call-done = f32[384,512]{1,0:T(8,128)} async-done(((f32[384,512]{1,0:T(8,128)}), f32[384,512]{1,0:T(8,128)}) %all-reduce.7.cloned.1.call-update) | async-done | bytes 786448 | tf_op jit(solution)/shard_map/psum | solution.py:82
  51.6 19.8 %all-gather.2.cloned.1.call-done = bf16[2048,512]{1,0:T(8,128)(2,1)} async-done(((bf16[256,512]{1,0:T(8,128)(2,1)}), bf16[2048,512]{1,0:T(8,128)(2,1)}) %all-gather.2.cloned.1.call-update) | async-done | bytes 2097168 | tf_op jit(solution)/shard_map/all_gather | solution.py:91
  71.4 4.2 %multiply_reduce_fusion = (f32[]{:T(128)}, f32[384,2048]{1,0:T(8,128)S(1)}) fusion(bf16[384,2048]{1,0:T(8,128)(2,1)} %param.15, bf16[2048,512]{1,0:T(8,128)(2,1)} %all-gather.2.cloned.1.call-done, f32[384,512]{1,0:T(8,128)} %all-reduce.7.cloned.1.call-done, f32[512]{0:T(512)S(1)} %copy-done.7), kind=kOutput, calls=%fused_computation.3 | convolution fusion | flops 809631744 | bytes 7604228 | tf_op jit(solution)/shard_map/dot_general | solution.py:21
  75.6 1.6 copy-done.1
  77.2 1.9 convolution_multiply_fusion.1
  79.2 5.3 %convolution_multiply_fusion = f32[2048,512]{1,0:T(8,128)} fusion(f32[384,2048]{1,0:T(8,128)} %copy-done.1, f32[384,512]{1,0:T(8,128)} %all-reduce.7.cloned.1.call-done, f32[512]{0:T(512)S(1)} %copy-done.7), kind=kOutput, calls=%fused_computation.1 | convolution fusion | flops 808321024 | bytes 8128512 | tf_op jit(solution)/shard_map/dot_general | solution.py:11
  84.6 28.1 %all-reduce.9.cloned.1.call-done = f32[384,512]{1,0:T(8,128)} async-done(((f32[384,512]{1,0:T(8,128)}), f32[384,512]{1,0:T(8,128)}) %all-reduce.9.cloned.1.call-update) | async-done | bytes 786448 | tf_op jit(solution)/shard_map/psum | solution.py:96
  112.8 2.1 fusion.28
  114.8 3.2 convolution_bitcast_fusion
  118.1 2.3 fusion.8
  120.5 51.0 %reduce-scatter.8.cloned.1.call-done = f32[256,512]{1,0:T(8,128)} async-done(((f32[2048,512]{1,0:T(8,128)}), f32[256,512]{1,0:T(8,128)}) %reduce-scatter.8.cloned.1.call-update) | async-done | bytes 524304 | tf_op jit(solution)/shard_map/reduce_scatter | solution.py:102
  171.5 1.8 fusion.27
  173.3 2.2 fusion.4
  175.5 1.3 fusion.13
  176.8 1.2 reduce_sum.56
  178.0 21.5 %all-reduce.2 = (f32[256]{0:T(256)}, f32[512]{0:T(512)}) all-reduce(f32[256]{0:T(256)S(1)} %copy-done.12, f32[512]{0:T(512)S(1)} %reduce_sum.56), channel_id=1, replica_groups=mesh['dp'=8,'query'=4] {'dp'}, use_global_device_ids=true, to_apply=%region_6.0 | all-reduce | flops 768 | bytes 6144 | tf_op jit(solution)/shard_map/psum | solution.py:111
  199.6 1.1 reduce_sum.59
  200.7 1.4 fusion.26
  202.5 38.7 %all-reduce = (f32[]{:T(128)}, f32[2,512]{1,0:T(2,128)}, f32[512]{0:T(512)}, f32[512]{0:T(512)}, f32[512]{0:T(512)}) all-reduce(f32[]{:T(128)} %get-tuple-element.35, f32[2,512]{1,0:T(2,128)S(1)} %fusion.29, f32[512]{0:T(512)S(1)} %get-tuple-element.37, ...), channel_id=1, replica_groups=mesh['dp'=8,'query'=4] {'dp','query'}, use_global_device_ids=true, to_apply=%region_2.0 | all-reduce | flops 2561 | bytes 20488 | tf_op jit(solution)/shard_map/psum | solution.py:100
  241.8 31.0 %reduce-scatter.4.cloned.1.call-done = f32[512,256]{0,1:T(8,128)} async-done(((f32[4096,256]{0,1:T(8,128)}), f32[512,256]{0,1:T(8,128)}) %reduce-scatter.4.cloned.1.call-update) | async-done | bytes 524304 | tf_op jit(solution)/shard_map/reduce_scatter | solution.py:115
  272.8 2.0 copy.24
  274.8 64.7 %reduce-scatter.6.cloned.1.call-done = f32[256,64]{0,1:T(8,128)} async-done(((f32[256,512]{0,1:T(8,128)}), f32[256,64]{0,1:T(8,128)}) %reduce-scatter.6.cloned.1.call-update) | async-done | bytes 65552 | tf_op jit(solution)/shard_map/reduce_scatter | solution.py:118
  339.5 3.7 %all-reduce.11.cloned.1.call-done = (f32[512,512]{1,0:T(8,128)}, f32[512,512]{1,0:T(8,128)}) async-done(((f32[512,512]{1,0:T(8,128)}, f32[512,512]{1,0:T(8,128)}), (f32[512,512]{1,0:T(8,128)}, f32[512,512]{1,0:T(8,128)})) %all-reduce.11.cloned.1.call-update) | async-done | bytes 2097168 | tf_op jit(solution)/shard_map/psum | solution.py:119
  343.2 2.3 copy.29
  345.5 2.3 copy.30
  (42 shorter events, 1.5 us)
Async XLA Ops:
  8.0 1.9 copy-start
  8.0 43.6 %all-reduce.7.cloned.1.call-start = ((), (), s32[]{:S(2)}) async-start(), calls=%async_computation.3 | async-start | bytes 1572864 | tf_op jit(solution)/shard_map/psum | solution.py:82
  9.9 2.6 copy-start.6
  12.5 58.9 %copy-start.7 = (f32[512]{0:T(512)S(1)}, f32[512]{0:T(512)}, u32[]{:S(2)}) copy-start(f32[512]{0:T(512)} %param.19) | copy-start | bytes 6148
  13.7 57.7 %all-gather.2.cloned.1.call-start = ((), (), s32[]{:S(2)}) async-start(), calls=%async_computation.4 | async-start | bytes 2359296 | tf_op jit(solution)/shard_map/all_gather | solution.py:91
  14.5 0.8 copy-start.8
  14.5 2.2 copy-start.10
  16.7 0.8 copy-start.2
  19.6 93.2 %all-reduce.9.cloned.1.call-start = ((), (), s32[]{:S(2)}) async-start(), calls=%async_computation.5 | async-start | bytes 1572864 | tf_op jit(solution)/shard_map/psum | solution.py:96
  71.4 5.8 %copy-start.5 = (bf16[2048,512]{1,0:T(8,128)(2,1)S(1)}, bf16[2048,512]{1,0:T(8,128)(2,1)}, u32[]{:S(2)}) copy-start(bf16[2048,512]{1,0:T(8,128)(2,1)} %all-gather.2.cloned.1.call-done) | copy-start | bytes 6291460
  75.6 1.6 copy-start.1
  79.1 92.3 %reduce-scatter.8.cloned.1.call-start = ((), (), s32[]{:S(2)}) async-start(), calls=%async_computation.8 | async-start | bytes 4718592 | tf_op jit(solution)/shard_map/reduce_scatter | solution.py:102
  84.5 188.2 %reduce-scatter.4.cloned.1.call-start = ((), (), s32[]{:S(2)}) async-start(), calls=%async_computation.6 | async-start | bytes 4718592 | tf_op jit(solution)/shard_map/reduce_scatter | solution.py:115
  118.0 55.2 %copy-start.9 = (f32[1,256]{1,0:T(1,128)S(1)}, f32[1,256]{1,0:T(1,128)}, u32[]{:S(2)}) copy-start(f32[1,256]{1,0:T(1,128)} %copy-done.8) | copy-start | bytes 3076
  118.1 221.4 %reduce-scatter.6.cloned.1.call-start = ((), (), s32[]{:S(2)}) async-start(), calls=%async_computation.7 | async-start | bytes 589824 | tf_op jit(solution)/shard_map/reduce_scatter | solution.py:118
  120.4 222.8 %all-reduce.11.cloned.1.call-start = ((), (), s32[]{:S(2)}) async-start(), calls=%async_computation.9 | async-start | bytes 4194304 | tf_op jit(solution)/shard_map/psum | solution.py:119
  171.5 4.0 %copy-start.3 = (f32[256,512]{1,0:T(8,128)S(1)}, f32[256,512]{1,0:T(8,128)}, u32[]{:S(2)}) copy-start(f32[256,512]{1,0:T(8,128)} %copy-done.2) | copy-start | bytes 1572868
  171.5 4.0 %copy-start.4 = (f32[256,512]{1,0:T(8,128)S(1)}, f32[256,512]{1,0:T(8,128)}, u32[]{:S(2)}) copy-start(f32[256,512]{1,0:T(8,128)} %reduce-scatter.8.cloned.1.call-done) | copy-start | bytes 1572868
  173.3 4.8 %copy-start.12 = (f32[256]{0:T(256)S(1)}, f32[256]{0:T(256)}, u32[]{:S(2)}) copy-start(f32[256]{0:T(256)} %get-tuple-element.41) | copy-start | bytes 3076
  173.3 27.4 %copy-start.11 = (f32[1,256]{1,0:T(1,128)S(1)}, f32[1,256]{1,0:T(1,128)}, u32[]{:S(2)}) copy-start(f32[1,256]{1,0:T(1,128)} %copy-done.10) | copy-start | bytes 3076
  173.3 27.4 %copy-start.13 = (f32[512]{0:T(512)S(1)}, f32[512]{0:T(512)}, u32[]{:S(2)}) copy-start(f32[512]{0:T(512)} %param.21) | copy-start | bytes 6148
Sparse Core Ops, SparseCore 0:
  13.9 37.7 all-reduce.6
  79.2 33.4 all-reduce.8
  176.9 166.2 all-reduce.10
Sparse Core Ops, SparseCore 1:
  19.7 51.7 all-gather.1
  84.6 86.8 reduce-scatter.7
  175.0 97.7 reduce-scatter.3
  276.7 62.7 reduce-scatter.5
where the time goes:
time: 357 us; the launch traced here: 356 us
  waiting for transfers between devices  230 us (64%)
  blocking collectives  60.2 us (17%)
  matrix products  33.3 us (9%)
  between operations  17.4 us (5%)
  local copies, waits for them, and re-layouts  11.7 us (3%)
    reduce_scatter x1, waiting for transfers between devices, local(): lax.psum_scatter(grad_w_two_part, 'dp', scatter_dimension=1, tiled=True)  64.7 us
    reduce_scatter x1, waiting for transfers between devices, local(): lax.psum_scatter(contract_rows(columns, coeffs_b) * inv_scale, 'dp', scat...  51 us
    psum x1, blocking collectives, local(): loss_value = lax.psum(loss_part, ('dp', 'query')) / count_all  38.7 us
    psum x1, waiting for transfers between devices, local(): coeffs = lax.psum(partial_value, 'query') + b_two  32 us
    reduce_scatter x1, waiting for transfers between devices, local(): lax.psum_scatter(contract_rows(columns, grad_pre_b), 'dp', scatter_dimens...  31 us
    psum x1, waiting for transfers between devices, local(): lax.psum(jnp.dot(misfit_b, basis_all, preferred_element_type=jnp.float32)...  28.1 us
    psum x1, blocking collectives, local(): lax.psum((jnp.sum(grad_pre, axis=0), jnp.sum(grad_coeffs, axis=0)), 'dp')  21.5 us
    all_gather x1, waiting for transfers between devices, local(): basis_all = lax.all_gather(basis_b, 'dp', axis=0, tiled=True)  19.8 us
  transfers between devices with their start and end apart: 7, of which 7 were waited for; matrix products, arithmetic and copies ran while one was open for 8% of the time, Pallas kernels for 0%

commit v1 on v0

--- a/solution.py
+++ b/solution.py
@@ -3,6 +3,7 @@
 import jax.numpy as jnp
 from jax import lax
 from jax.sharding import PartitionSpec as P
+from jax.lax import all_to_all, axis_size
 
 GRID = 128
 
@@ -88,7 +89,11 @@
     first_act, first_b, second_act, second_b, basis_b = trunk_forward(
         coords_mine, v_one, c_one, v_two, c_two, v_three, c_three
     )
-    basis_all = lax.all_gather(basis_b, "dp", axis=0, tiled=True)
+
+    def attach_the_spots(z_in):
+        return jnp.concatenate(all_to_all(jnp.stack([z_in] * axis_size("dp")), "dp", 0, 0), 0)
+
+    basis_all = attach_the_spots(basis_b)
     prediction = contract_cols(coeffs_b, basis_all) * inv_scale
     misfit = prediction - targets.astype(jnp.float32)
     loss_part = jnp.sum(misfit * misfit)

time: 357 us -> 517 us (1.45)
  waiting for transfers between devices: 230 us -> 385 us
  starting transfers between devices: 0.3 us -> 7.56 us
    psum x1, waiting for transfers between devices: 3.7 us -> 140 us  [local(): lax.psum((trunk_parts[0], trunk_parts[1], trunk_parts[2], trunk_parts[3],...]
    reduce_scatter x1, waiting for transfers between devices: 51 us -> 84.2 us  [local(): lax.psum_scatter(contract_rows(columns, coeffs_b) * inv_scale, 'dp', scat...]
    all_gather x1 -> x0, waiting for transfers between devices: 19.8 us -> none  [local(): basis_all = lax.all_gather(basis_b, 'dp', axis=0, tiled=True)]
    all_to_all x0 -> x1, waiting for transfers between devices: none -> 8.08 us  [attach_the_spots(): all_to_all(jnp.stack([z_in] * axis_size('dp')), 'dp', 0, 0)]
    reduce_scatter x1, waiting for transfers between devices: 31 us -> 23.6 us  [local(): lax.psum_scatter(contract_rows(columns, grad_pre_b), 'dp', scatter_dimens...]
    all_to_all x0 -> x1, starting transfers between devices: none -> 7.31 us  [attach_the_spots(): all_to_all(jnp.stack([z_in] * axis_size('dp')), 'dp', 0, 0)]
    unnamed x31 -> x29, local copies, waits for them, and re-layouts: 10.9 us -> 9.06 us
  transfers between devices with their start and end apart: 7 -> 7, of which waited for: 7 -> 7; matrix products, arithmetic and copies ran while one was open for 8% -> 5% of each run, Pallas kernels for 0% -> 0%
where the time goes in v1:
time: 517 us; the launch traced here: 516 us
  waiting for transfers between devices  385 us (74%)
  blocking collectives  58.6 us (11%)
  matrix products  34 us (7%)
  between operations  16 us (3%)
  local copies, waits for them, and re-layouts  11.4 us (2%)
  starting transfers between devices  7.56 us (1%)
    psum x1, waiting for transfers between devices, local(): lax.psum((trunk_parts[0], trunk_parts[1], trunk_parts[2], trunk_parts[3],...  140 us
    reduce_scatter x1, waiting for transfers between devices, local(): lax.psum_scatter(contract_rows(columns, coeffs_b) * inv_scale, 'dp', scat...  84.2 us
    reduce_scatter x1, waiting for transfers between devices, local(): lax.psum_scatter(grad_w_two_part, 'dp', scatter_dimension=1, tiled=True)  64 us
    psum x1, blocking collectives, local(): loss_value = lax.psum(loss_part, ('dp', 'query')) / count_all  37.1 us
    psum x1, waiting for transfers between devices, local(): coeffs = lax.psum(partial_value, 'query') + b_two  36.3 us
    psum x1, waiting for transfers between devices, local(): lax.psum(jnp.dot(misfit_b, basis_all, preferred_element_type=jnp.float32)...  28.8 us
    reduce_scatter x1, waiting for transfers between devices, local(): lax.psum_scatter(contract_rows(columns, grad_pre_b), 'dp', scatter_dimens...  23.6 us
    psum x1, blocking collectives, local(): lax.psum((jnp.sum(grad_pre, axis=0), jnp.sum(grad_coeffs, axis=0)), 'dp')  21.5 us
  transfers between devices with their start and end apart: 7, of which 7 were waited for; matrix products, arithmetic and copies ran while one was open for 5% of the time, Pallas kernels for 0%

profile of v1, /device:TPU:0, one launch (start us, length us, event | category | flops | bytes accessed | tf_op | source)
XLA Modules:
  0.0 516.0 jit_solution(6884047799347011229)
XLA Ops:
  7.2 0.8 fusion.21
  8.9 1.4 fusion
  11.1 1.4 fusion.1
  12.5 1.5 stack.2
  14.0 7.3 %all-to-all-start = ((bf16[8,256,512]{2,1,0:T(8,128)(2,1)}), bf16[8,256,512]{2,1,0:T(8,128)(2,1)}, u32[]{:S(2)}, u32[]{:S(2)}) async-start(bf16[8,256,512]{2,1,0:T(8,128)(2,1)} %stack.2), calls=%async_computation | async-start | bytes 4194304 | tf_op jit(solution)/shard_map/all_to_all | solution.py:94
  21.4 2.6 fusion.2
  24.0 1.1 fusion.19
  25.2 36.3 %all-reduce.7.cloned.1.call-done = f32[384,512]{1,0:T(8,128)} async-done(((f32[384,512]{1,0:T(8,128)}), f32[384,512]{1,0:T(8,128)}) %all-reduce.7.cloned.1.call-update) | async-done | bytes 786448 | tf_op jit(solution)/shard_map/psum | solution.py:83
  61.6 8.1 %all-to-all-done = bf16[8,256,512]{2,1,0:T(8,128)(2,1)} async-done(((bf16[8,256,512]{2,1,0:T(8,128)(2,1)}), bf16[8,256,512]{2,1,0:T(8,128)(2,1)}, u32[]{:S(2)}, u32[]{:S(2)}) %all-to-all-start) | async-done | bytes 2097184 | tf_op jit(solution)/shard_map/all_to_all | solution.py:94
  69.6 4.0 multiply_reduce_fusion
  73.7 1.7 copy-done.1
  75.3 3.4 convolution_multiply_fusion.1
  78.8 5.3 %convolution_multiply_fusion = f32[2048,512]{1,0:T(8,128)} fusion(f32[384,2048]{1,0:T(8,128)} %copy-done.1, f32[384,512]{1,0:T(8,128)} %all-reduce.7.cloned.1.call-done, f32[512]{0:T(512)S(1)} %copy-done.6), kind=kOutput, calls=%fused_computation.1 | convolution fusion | flops 808321024 | bytes 8128512 | tf_op jit(solution)/shard_map/dot_general | solution.py:12
  84.2 28.8 %all-reduce.9.cloned.1.call-done = f32[384,512]{1,0:T(8,128)} async-done(((f32[384,512]{1,0:T(8,128)}), f32[384,512]{1,0:T(8,128)}) %all-reduce.9.cloned.1.call-update) | async-done | bytes 786448 | tf_op jit(solution)/shard_map/psum | solution.py:101
  113.0 2.1 fusion.28
  115.1 3.2 convolution_bitcast_fusion
  118.4 2.3 fusion.8
  120.7 84.2 %reduce-scatter.8.cloned.1.call-done = f32[256,512]{1,0:T(8,128)} async-done(((f32[2048,512]{1,0:T(8,128)}), f32[256,512]{1,0:T(8,128)}) %reduce-scatter.8.cloned.1.call-update) | async-done | bytes 524304 | tf_op jit(solution)/shard_map/reduce_scatter | solution.py:107
  205.0 1.8 fusion.27
  206.8 2.2 fusion.4
  209.0 1.3 fusion.13
  210.3 1.2 reduce_sum.56
  211.5 21.5 %all-reduce.2 = (f32[256]{0:T(256)}, f32[512]{0:T(512)}) all-reduce(f32[256]{0:T(256)S(1)} %copy-done.11, f32[512]{0:T(512)S(1)} %reduce_sum.56), channel_id=1, replica_groups=mesh['dp'=8,'query'=4] {'dp'}, use_global_device_ids=true, to_apply=%region_6.0 | all-reduce | flops 768 | bytes 6144 | tf_op jit(solution)/shard_map/psum | solution.py:116
  233.0 1.1 reduce_sum.59
  234.1 1.4 fusion.26
  235.9 37.1 %all-reduce = (f32[]{:T(128)}, f32[2,512]{1,0:T(2,128)}, f32[512]{0:T(512)}, f32[512]{0:T(512)}, f32[512]{0:T(512)}) all-reduce(f32[]{:T(128)} %get-tuple-element.35, f32[2,512]{1,0:T(2,128)S(1)} %fusion.29, f32[512]{0:T(512)S(1)} %get-tuple-element.37, ...), channel_id=1, replica_groups=mesh['dp'=8,'query'=4] {'dp','query'}, use_global_device_ids=true, to_apply=%region_2.0 | all-reduce | flops 2561 | bytes 20488 | tf_op jit(solution)/shard_map/psum | solution.py:105
  273.6 23.6 %reduce-scatter.4.cloned.1.call-done = f32[512,256]{0,1:T(8,128)} async-done(((f32[4096,256]{0,1:T(8,128)}), f32[512,256]{0,1:T(8,128)}) %reduce-scatter.4.cloned.1.call-update) | async-done | bytes 524304 | tf_op jit(solution)/shard_map/reduce_scatter | solution.py:120
  297.2 2.0 copy.24
  299.3 64.0 %reduce-scatter.6.cloned.1.call-done = f32[256,64]{0,1:T(8,128)} async-done(((f32[256,512]{0,1:T(8,128)}), f32[256,64]{0,1:T(8,128)}) %reduce-scatter.6.cloned.1.call-update) | async-done | bytes 65552 | tf_op jit(solution)/shard_map/reduce_scatter | solution.py:123
  363.2 140.2 %all-reduce.11.cloned.1.call-done = (f32[512,512]{1,0:T(8,128)}, f32[512,512]{1,0:T(8,128)}) async-done(((f32[512,512]{1,0:T(8,128)}, f32[512,512]{1,0:T(8,128)}), (f32[512,512]{1,0:T(8,128)}, f32[512,512]{1,0:T(8,128)})) %all-reduce.11.cloned.1.call-update) | async-done | bytes 2097168 | tf_op jit(solution)/shard_map/psum | solution.py:124
  503.5 2.3 copy.29
  505.7 2.3 copy.30
  (40 shorter events, 2.4 us)
Async XLA Ops:
  7.2 14.2 %copy-start = (bf16[384,4096]{1,0:T(8,128)(2,1)S(1)}, bf16[384,4096]{1,0:T(8,128)(2,1)}, u32[]{:S(2)}) copy-start(bf16[384,4096]{1,0:T(8,128)(2,1)} %param.13) | copy-start | bytes 9437188
  8.0 0.8 copy-start.7
  8.0 2.3 copy-start.9
  10.3 0.8 copy-start.2
  14.0 55.6 %all-to-all-start = ((bf16[8,256,512]{2,1,0:T(8,128)(2,1)}), bf16[8,256,512]{2,1,0:T(8,128)(2,1)}, u32[]{:S(2)}, u32[]{:S(2)}) async-start(bf16[8,256,512]{2,1,0:T(8,128)(2,1)} %stack.2), calls=%async_computation | async-start | bytes 4194304 | tf_op jit(solution)/shard_map/all_to_all | solution.py:94
  21.3 48.3 %copy-start.6 = (f32[512]{0:T(512)S(1)}, f32[512]{0:T(512)}, u32[]{:S(2)}) copy-start(f32[512]{0:T(512)} %param.19) | copy-start | bytes 6148
  21.3 40.3 %all-reduce.7.cloned.1.call-start = ((), (), s32[]{:S(2)}) async-start(), calls=%async_computation.4 | async-start | bytes 1572864 | tf_op jit(solution)/shard_map/psum | solution.py:83
  21.4 2.6 copy-start.5
  25.2 87.8 %all-reduce.9.cloned.1.call-start = ((), (), s32[]{:S(2)}) async-start(), calls=%async_computation.5 | async-start | bytes 1572864 | tf_op jit(solution)/shard_map/psum | solution.py:101
  73.7 1.7 copy-start.1
  78.8 126.2 %reduce-scatter.8.cloned.1.call-start = ((), (), s32[]{:S(2)}) async-start(), calls=%async_computation.8 | async-start | bytes 4718592 | tf_op jit(solution)/shard_map/reduce_scatter | solution.py:107
  84.2 213.0 %reduce-scatter.4.cloned.1.call-start = ((), (), s32[]{:S(2)}) async-start(), calls=%async_computation.6 | async-start | bytes 4718592 | tf_op jit(solution)/shard_map/reduce_scatter | solution.py:120
  118.3 88.5 %copy-start.8 = (f32[1,256]{1,0:T(1,128)S(1)}, f32[1,256]{1,0:T(1,128)}, u32[]{:S(2)}) copy-start(f32[1,256]{1,0:T(1,128)} %copy-done.7) | copy-start | bytes 3076
  118.3 244.9 %reduce-scatter.6.cloned.1.call-start = ((), (), s32[]{:S(2)}) async-start(), calls=%async_computation.7 | async-start | bytes 589824 | tf_op jit(solution)/shard_map/reduce_scatter | solution.py:123
  120.7 382.8 %all-reduce.11.cloned.1.call-start = ((), (), s32[]{:S(2)}) async-start(), calls=%async_computation.9 | async-start | bytes 4194304 | tf_op jit(solution)/shard_map/psum | solution.py:124
  205.0 4.0 copy-start.3
  205.0 4.0 copy-start.4
  206.8 4.8 copy-start.11
  206.8 27.3 %copy-start.10 = (f32[1,256]{1,0:T(1,128)S(1)}, f32[1,256]{1,0:T(1,128)}, u32[]{:S(2)}) copy-start(f32[1,256]{1,0:T(1,128)} %copy-done.9) | copy-start | bytes 3076
  206.8 27.3 %copy-start.12 = (f32[512]{0:T(512)S(1)}, f32[512]{0:T(512)}, u32[]{:S(2)}) copy-start(f32[512]{0:T(512)} %param.21) | copy-start | bytes 6148
Sparse Core Ops, SparseCore 0:
  25.3 36.2 all-reduce.6
  78.9 34.0 all-reduce.8
  116.6 88.2 reduce-scatter.7
  208.4 88.7 reduce-scatter.3
  301.0 62.2 reduce-scatter.5
  369.8 133.6 all-reduce.10
